TPU v7x, 32 devices: a whole 2x2x4 slice. The times are simulated.
32 devices in a mesh: dp: 8 (over z, y), mp: 4 (over x, core).
Axes of the slice: x: 2, y: 2, z: 4, core: 2. Of those that a mesh axis runs over, the one named last changes fastest.
Arguments:
- logits: bfloat16 [1024, 16384], P('dp', 'mp'), may hold values from -72 to 240
- targets: int32 [1024], P('dp'), may hold values from 0 to 16383
- resp_mask: int32 [1024], P('dp'), may hold values from 0 to 1, as said below
- rewards: int32 [8], P('dp'), may hold values from 0 to 10
- groups: int32 [8], P('dp'), may hold values from 0 to 1, as said below
- unit_grad: bfloat16 [1024, 8192], P(('dp', 'mp')), may hold values from -192 to 192
- mix: bfloat16 [1024, 2048], P('dp', 'mp'), may hold values from -6 to 6
- w_out: bfloat16 [2048, 8192], P('mp', 'dp'), may hold values from -0.125 to 0.125
Outputs:
- token_logprob: float32 [1024], P('dp')
- policy_loss: float32 [], replicated
- grad_mix: bfloat16 [1024, 2048], P('dp', 'mp')
- grad_w_out: bfloat16 [2048, 8192], P('mp', 'dp')
Inputs may be any that keep to these rules, and one draw needn't show every extreme that they name: `resp_mask`: in each sample the response mask is a run of ones followed by zeros, with at least 32 ones. `groups`: each prompt id names exactly 4 samples.
All inputs are finite; a program needn't handle non-finite values.
Results may differ from a plain program's by a relative error of at most 0.005.
Values may be sent and summed in bfloat16 or wider, within the bound.
A program may use at most 64 MiB of HBM per device.

v0:
```python
import jax
import jax.numpy as jnp
from jax import lax
from jax.sharding import PartitionSpec as P

K = 4


def shards(logits, targets, resp_mask, rewards, groups, unit_grad, mix, w_out):
    tok_rows, vocab_dev = logits.shape
    mp_lane = lax.axis_index("mp")
    local_target = targets - mp_lane * vocab_dev
    present = (local_target >= 0) & (local_target < vocab_dev)
    picked = jnp.take_along_axis(logits, jnp.clip(local_target, 0, vocab_dev - 1)[:, None], axis=1)[
        :, 0
    ]
    picked = jnp.where(present, picked.astype(jnp.float32), 0.0)
    local_max = jnp.max(logits, axis=1).astype(jnp.float32)
    highest = lax.pmax(local_max, "mp")
    local_sum = jnp.sum(jnp.exp(logits.astype(jnp.float32) - highest[:, None]), axis=1)
    summed, target_logit = lax.psum((local_sum, picked), "mp")
    logprob = target_logit - (highest + jnp.log(summed))
    mask_float = resp_mask.astype(jnp.float32)
    local_count = jnp.sum(mask_float)
    reward_float = rewards.astype(jnp.float32)
    prompt_slots = jnp.arange(lax.axis_size("dp") // K, dtype=jnp.int32)
    own_slot = (prompt_slots == groups[0]).astype(jnp.float32)
    group_total, token_count = lax.psum((own_slot * reward_float[0], local_count), "dp")
    own_total = jnp.sum(own_slot * group_total)
    advantage = reward_float[0] - (own_total - reward_float[0]) / (K - 1)
    weight = advantage * mask_float / token_count
    policy_loss = lax.psum(-jnp.sum(weight * logprob), "dp")
    sub_rows = unit_grad.shape[0]
    part_weight = lax.dynamic_slice_in_dim(weight, mp_lane * sub_rows, sub_rows)
    grad_local = (-part_weight[:, None] * unit_grad.astype(jnp.float32)).astype(jnp.bfloat16)
    grad_group = lax.all_gather(grad_local, "mp", axis=0, tiled=True)
    grad_mix = lax.dot_general(
        grad_group,
        lax.all_gather(w_out, "dp", axis=1, tiled=True),
        (((1,), (1,)), ((), ())),
        preferred_element_type=jnp.float32,
    ).astype(jnp.bfloat16)
    grad_every = lax.all_to_all(grad_group, "dp", split_axis=1, concat_axis=0, tiled=True)
    grad_w_out = lax.dot_general(
        lax.all_gather(mix, "dp", axis=0, tiled=True),
        grad_every,
        (((0,), (0,)), ((), ())),
        preferred_element_type=jnp.float32,
    ).astype(jnp.bfloat16)
    return (logprob, policy_loss, grad_mix, grad_w_out)


def solution(mesh):
    return jax.shard_map(
        shards,
        mesh=mesh,
        in_specs=(
            P("dp", "mp"),
            P("dp"),
            P("dp"),
            P("dp"),
            P("dp"),
            P(("dp", "mp"), None),
            P("dp", "mp"),
            P("mp", "dp"),
        ),
        out_specs=(P("dp"), P(), P("dp", "mp"), P("mp", "dp")),
        check_vma=False,
    )
```

profile of v0, /device:TPU:0, one launch (start us, length us, event | category | flops | bytes accessed | tf_op | source)
XLA Modules:
  0.0 279.9 jit_solution(4905215738061434298)
XLA Ops:
  7.2 0.0 copy-start.2
  7.2 0.0 copy-start.1
  7.2 0.0 all-gather.4.cloned.1.call-start
  7.2 1.3 convert_reduce_fusion
  9.9 23.8 %all-reduce = (f32[]{:T(128)}, f32[2]{0:T(128)S(1)}) all-reduce(f32[]{:T(128)} %convert_reduce_fusion, f32[2]{0:T(128)S(1)} %compare_select_fusion.2), channel_id=1, replica_groups=mesh['dp'=8,'mp'=4] {'dp'}, use_global_device_ids=true, to_apply=%region_8.9 | all-reduce | flops 3 | bytes 24 | tf_op jit(solution)/shard_map/psum | solution.py:28
  33.6 0.6 fusion.1
  34.9 0.7 fusion.2
  35.6 2.3 gather_fusion
  37.9 0.7 and_select_fusion.1
  38.5 1.4 reduce_max.9
  40.0 5.7 %pmax.7 = f32[128]{0:T(128)S(1)} all-reduce(bf16[128]{0:T(256)(128)(2,1)S(1)} %reduce_max.9), channel_id=1, replica_groups=mesh['dp'=8,'mp'=4] {'mp'}, use_global_device_ids=true, to_apply=%region_2.3 | all-reduce | flops 128 | bytes 768 | tf_op jit(solution)/shard_map/pmax | solution.py:19
  45.6 1.7 exponential_reduce_fusion
  47.4 6.6 %all-reduce.1 = (f32[128]{0:T(128)S(1)}, f32[128]{0:T(128)S(1)}) all-reduce(f32[128]{0:T(128)S(1)} %and_select_fusion.1, f32[128]{0:T(128)S(1)} %exponential_reduce_fusion), channel_id=1, replica_groups=mesh['dp'=8,'mp'=4] {'mp'}, use_global_device_ids=true, to_apply=%region_0.1 | all-reduce | flops 256 | bytes 2048 | tf_op jit(solution)/shard_map/psum | solution.py:21
  53.9 0.0 copy-done.2
  53.9 1.8 multiply_reduce_fusion
  55.7 0.1 dynamic-slice_negate_fusion
  55.8 0.0 copy-done.1
  55.8 0.9 multiply_convert_fusion
  56.7 0.0 all-gather.4.cloned.1.call-update
  56.7 0.0 all-gather.8.cloned.1.call-start
  56.8 0.7 all-gather.8.cloned.1.call-update
  57.5 0.0 all-gather.6.cloned.1.call-start
  57.5 0.7 all-gather.6.cloned.1.call-update
  58.2 18.0 %all-gather.4.cloned.1.call-done = bf16[128,8192]{1,0:T(8,128)(2,1)} async-done(((bf16[32,8192]{1,0:T(8,128)(2,1)}), bf16[128,8192]{1,0:T(8,128)(2,1)}) %all-gather.4.cloned.1.call-update) | async-done | bytes 2097168 | tf_op jit(solution)/shard_map/all_gather | solution.py:36
  76.2 4.1 %copy.17 = bf16[128,8192]{0,1:T(8,128)(2,1)} copy(bf16[128,8192]{1,0:T(8,128)(2,1)} %all-gather.4.cloned.1.call-done) | data formatting | bytes 4194304 | tf_op jit(solution)/shard_map/all_gather | solution.py:36
  80.3 5.5 %all-to-all-start = ((bf16[128,8,1024]{0,2,1:T(8,128)(2,1)}), bf16[128,8,1024]{0,2,1:T(8,128)(2,1)S(1)}, u32[]{:S(2)}, u32[]{:S(2)}) async-start(bf16[128,8,1024]{0,2,1:T(8,128)(2,1)} %bitcast.20), calls=%async_computation | async-start | bytes 4194304 | tf_op jit(solution)/shard_map/all_to_all | solution.py:43
  86.4 56.0 %psum.39 = f32[]{:T(128)} all-reduce(f32[]{:T(128)S(6)} %neg.7), channel_id=1, replica_groups=mesh['dp'=8,'mp'=4] {'dp'}, use_global_device_ids=true, to_apply=%region_10.11 | all-reduce | flops 1 | bytes 8 | tf_op jit(solution)/shard_map/psum | solution.py:32
  142.5 4.6 %all-to-all-done = bf16[128,8,1024]{0,2,1:T(8,128)(2,1)S(1)} async-done(((bf16[128,8,1024]{0,2,1:T(8,128)(2,1)}), bf16[128,8,1024]{0,2,1:T(8,128)(2,1)S(1)}, u32[]{:S(2)}, u32[]{:S(2)}) %all-to-all-start) | async-done | bytes 2097184 | tf_op jit(solution)/shard_map/all_to_all | solution.py:43
  147.1 2.6 copy.18
  149.7 0.0 all-gather.8.cloned.1.call-done
  149.7 3.4 %fusion = bf16[512,1024]{0,1:T(8,128)(2,1)S(1)} fusion(bf16[1024,1024]{1,0:T(8,128)(2,1)} %bitcast.21, bf16[1024,512]{1,0:T(8,128)(2,1)} %all-gather.8.cloned.1.call-done), kind=kOutput, calls=%fused_computation.3 | convolution fusion | flops 1074266112 | bytes 4194304 | tf_op jit(solution)/shard_map/dot_general | solution.py:44
  153.1 0.0 copy-start
  153.1 1.3 copy.19
  154.4 112.0 %all-gather.6.cloned.1.call-done = bf16[512,8192]{1,0:T(8,128)(2,1)} async-done(((bf16[512,1024]{1,0:T(8,128)(2,1)}), bf16[512,8192]{1,0:T(8,128)(2,1)}) %all-gather.6.cloned.1.call-update) | async-done | bytes 8388624 | tf_op jit(solution)/shard_map/all_gather | solution.py:39
  266.4 0.0 copy-done
  266.4 7.0 %convolution_convert_fusion.1 = bf16[128,512]{1,0:T(8,128)(2,1)} fusion(bf16[128,8192]{1,0:T(8,128)(2,1)S(1)} %copy-done, bf16[512,8192]{1,0:T(8,128)(2,1)} %all-gather.6.cloned.1.call-done), kind=kOutput, calls=%fused_computation.4 | convolution fusion | flops 1073807360 | bytes 10616832 | tf_op jit(solution)/shard_map/dot_general | solution.py:37
  (4 shorter events, 0.0 us)
Async XLA Ops:
  7.2 46.8 %copy-start.2 = (s32[128]{0:T(128)S(1)}, s32[128]{0:T(128)}, u32[]{:S(2)}) copy-start(s32[128]{0:T(128)} %param.10) | copy-start | bytes 1540
  7.2 48.6 %copy-start.1 = (bf16[32,8192]{1,0:T(8,128)(2,1)S(1)}, bf16[32,8192]{1,0:T(8,128)(2,1)}, u32[]{:S(2)}) copy-start(bf16[32,8192]{1,0:T(8,128)(2,1)} %param.13) | copy-start | bytes 1572868
  7.2 69.0 %all-gather.4.cloned.1.call-start = ((), (), s32[]{:S(2)}) async-start(), calls=%async_computation.1 | async-start | bytes 2621440 | tf_op jit(solution)/shard_map/all_gather | solution.py:36
  56.7 92.9 %all-gather.8.cloned.1.call-start = ((), (), s32[]{:S(2)}) async-start(), calls=%async_computation.3 | async-start | bytes 1179648 | tf_op jit(solution)/shard_map/all_gather | solution.py:45
  57.5 208.9 %all-gather.6.cloned.1.call-start = ((), (), s32[]{:S(2)}) async-start(), calls=%async_computation.2 | async-start | bytes 9437184 | tf_op jit(solution)/shard_map/all_gather | solution.py:39
  80.3 66.8 %all-to-all-start = ((bf16[128,8,1024]{0,2,1:T(8,128)(2,1)}), bf16[128,8,1024]{0,2,1:T(8,128)(2,1)S(1)}, u32[]{:S(2)}, u32[]{:S(2)}) async-start(bf16[128,8,1024]{0,2,1:T(8,128)(2,1)} %bitcast.20), calls=%async_computation | async-start | bytes 4194304 | tf_op jit(solution)/shard_map/all_to_all | solution.py:43
  153.1 113.3 %copy-start = (bf16[128,8192]{1,0:T(8,128)(2,1)S(1)}, bf16[128,8192]{1,0:T(8,128)(2,1)}, u32[]{:S(2)}) copy-start(bf16[128,8192]{1,0:T(8,128)(2,1)} %all-gather.4.cloned.1.call-done) | copy-start | bytes 6291460
Sparse Core Ops, SparseCore 0:
  56.9 19.2 all-gather.3
  78.3 63.1 all-gather.7
  143.7 122.6 all-gather.5
where the time goes:
time: 280 us
  waiting for transfers between devices  136 us (49%)
  blocking collectives  92 us (33%)
  between operations  16.4 us (6%)
  matrix products  10.4 us (4%)
  local copies, waits for them, and re-layouts  10.3 us (4%)
  other arithmetic  9.22 us (3%)
  starting transfers between devices  5.63 us (2%)
    all_gather x1, waiting for transfers between devices, shards(): lax.all_gather(w_out, 'dp', axis=1, tiled=True)  112 us
    psum x1, blocking collectives, shards(): policy_loss = lax.psum(-jnp.sum(weight * logprob), 'dp')  56 us
    psum x1, blocking collectives, shards(): lax.psum((own_slot * reward_float[0], local_count), 'dp')  23.8 us
    all_gather x1, waiting for transfers between devices, shards(): grad_group = lax.all_gather(grad_local, 'mp', axis=0, tiled=True)  18 us
    dot_general x1, matrix products, shards(): lax.dot_general(grad_group, lax.all_gather(w_out, 'dp', axis=1, tiled=Tru...  6.96 us
    psum x1, blocking collectives, shards(): summed, target_logit = lax.psum((local_sum, picked), 'mp')  6.56 us
    pmax x1, blocking collectives, shards(): highest = lax.pmax(local_max, 'mp')  5.66 us
  transfers between devices with their start and end apart: 4, of which 3 were waited for; matrix products, arithmetic and copies ran while one was open for 4% of the time, Pallas kernels for 0%

commit v1 on v0

--- a/solution.py
+++ b/solution.py
@@ -7,6 +7,20 @@
 
 
 def shards(logits, targets, resp_mask, rewards, groups, unit_grad, mix, w_out):
+
+    def shapes_load(row_data):
+        p_count = jax.lax.axis_size("mp")
+        r1 = sorted(((j0, (j0 + 1) % p_count) for j0 in range(p_count)))
+        latest = row_data
+        views = [latest]
+        for b in range(1, p_count):
+            latest = jax.lax.ppermute(latest, "mp", r1)
+            views.insert(0, latest)
+        arr_now = jnp.concatenate(views, axis=0)
+        carry = jax.lax.axis_index("mp") + 1
+        carry_out = jnp.roll(arr_now, shift=carry * row_data.shape[0], axis=0)
+        return carry_out
+
     tok_rows, vocab_dev = logits.shape
     mp_lane = lax.axis_index("mp")
     local_target = targets - mp_lane * vocab_dev
@@ -33,7 +47,7 @@
     sub_rows = unit_grad.shape[0]
     part_weight = lax.dynamic_slice_in_dim(weight, mp_lane * sub_rows, sub_rows)
     grad_local = (-part_weight[:, None] * unit_grad.astype(jnp.float32)).astype(jnp.bfloat16)
-    grad_group = lax.all_gather(grad_local, "mp", axis=0, tiled=True)
+    grad_group = shapes_load(grad_local)
     grad_mix = lax.dot_general(
         grad_group,
         lax.all_gather(w_out, "dp", axis=1, tiled=True),

time: 280 us -> 240 us (0.86)
  waiting for transfers between devices: 136 us -> 83.4 us
  blocking collectives: 92 us -> 104 us
    all_gather x1, waiting for transfers between devices: 112 us -> 26.4 us  [shards(): lax.all_gather(w_out, 'dp', axis=1, tiled=True)]
    all_to_all x1, waiting for transfers between devices: 4.61 us -> 30.5 us  [shards(): lax.all_to_all(grad_group, 'dp', split_axis=1, concat_axis=0, tiled=True)]
    ppermute x0 -> x3, waiting for transfers between devices: none -> 25.8 us  [shapes_load(): latest = jax.lax.ppermute(latest, 'mp', r1)]
    all_gather x1 -> x0, waiting for transfers between devices: 18 us -> none  [shards(): grad_group = lax.all_gather(grad_local, 'mp', axis=0, tiled=True)]
    psum x1, blocking collectives: 56 us -> 67.1 us  [shards(): policy_loss = lax.psum(-jnp.sum(weight * logprob), 'dp')]
    all_gather x1 -> x0, local copies, waits for them, and re-layouts: 4.07 us -> none  [shards(): grad_group = lax.all_gather(grad_local, 'mp', axis=0, tiled=True)]
  transfers between devices with their start and end apart: 4 -> 6, of which waited for: 3 -> 5; matrix products, arithmetic and copies ran while one was open for 4% -> 10% of each run, Pallas kernels for 0% -> 0%
where the time goes in v1:
time: 240 us; the launch traced here: 239 us
  blocking collectives  104 us (43%)
  waiting for transfers between devices  83.4 us (35%)
  between operations  16.8 us (7%)
  local copies, waits for them, and re-layouts  10.4 us (4%)
  other arithmetic  10.4 us (4%)
  matrix products  10.2 us (4%)
  starting transfers between devices  4.49 us (2%)
    psum x1, blocking collectives, shards(): policy_loss = lax.psum(-jnp.sum(weight * logprob), 'dp')  67.1 us
    all_to_all x1, waiting for transfers between devices, shards(): lax.all_to_all(grad_group, 'dp', split_axis=1, concat_axis=0, tiled=True)  30.5 us
    all_gather x1, waiting for transfers between devices, shards(): lax.all_gather(w_out, 'dp', axis=1, tiled=True)  26.4 us
    ppermute x3, waiting for transfers between devices, shapes_load(): latest = jax.lax.ppermute(latest, 'mp', r1)  25.8 us
    psum x1, blocking collectives, shards(): lax.psum((own_slot * reward_float[0], local_count), 'dp')  23.9 us
    dot_general x1, matrix products, shards(): lax.dot_general(grad_group, lax.all_gather(w_out, 'dp', axis=1, tiled=Tru...  6.96 us
    psum x1, blocking collectives, shards(): summed, target_logit = lax.psum((local_sum, picked), 'mp')  6.67 us
    pmax x1, blocking collectives, shards(): highest = lax.pmax(local_max, 'mp')  6.06 us
  transfers between devices with their start and end apart: 6, of which 5 were waited for; matrix products, arithmetic and copies ran while one was open for 10% of the time, Pallas kernels for 0%

profile of v1, /device:TPU:0, one launch (start us, length us, event | category | flops | bytes accessed | tf_op | source)
XLA Modules:
  0.0 239.4 jit_solution(13465192785727842736)
XLA Ops:
  7.2 0.0 copy-start
  7.2 0.0 all-gather.5.cloned.1.call-start
  7.2 0.7 all-gather.5.cloned.1.call-update
  7.9 0.0 all-gather.3.cloned.1.call-start
  8.0 1.3 convert_reduce_fusion
  10.5 23.9 %all-reduce = (f32[]{:T(128)}, f32[2]{0:T(128)S(1)}) all-reduce(f32[]{:T(128)} %convert_reduce_fusion, f32[2]{0:T(128)S(1)} %compare_select_fusion.2), channel_id=1, replica_groups=mesh['dp'=8,'mp'=4] {'dp'}, use_global_device_ids=true, to_apply=%region_8.9 | all-reduce | flops 3 | bytes 24 | tf_op jit(solution)/shard_map/psum | solution.py:42
  34.4 0.6 fusion.1
  35.7 0.7 fusion.2
  36.4 2.3 gather_fusion
  38.7 0.7 and_select_fusion.1
  39.3 1.4 reduce_max.9
  40.8 6.1 %pmax.7 = f32[128]{0:T(128)S(1)} all-reduce(bf16[128]{0:T(256)(128)(2,1)S(1)} %reduce_max.9), channel_id=1, replica_groups=mesh['dp'=8,'mp'=4] {'mp'}, use_global_device_ids=true, to_apply=%region_2.3 | all-reduce | flops 128 | bytes 768 | tf_op jit(solution)/shard_map/pmax | solution.py:33
  46.9 1.7 exponential_reduce_fusion
  48.6 6.7 %all-reduce.1 = (f32[128]{0:T(128)S(1)}, f32[128]{0:T(128)S(1)}) all-reduce(f32[128]{0:T(128)S(1)} %and_select_fusion.1, f32[128]{0:T(128)S(1)} %exponential_reduce_fusion), channel_id=1, replica_groups=mesh['dp'=8,'mp'=4] {'mp'}, use_global_device_ids=true, to_apply=%region_0.1 | all-reduce | flops 256 | bytes 2048 | tf_op jit(solution)/shard_map/psum | solution.py:35
  55.3 2.4 %multiply_reduce_fusion = (f32[]{:T(128)}, f32[128]{0:T(128)S(1)}, f32[128]{0:T(128)}) fusion(f32[]{:T(128)} %get-tuple-element.24, s32[128]{0:T(128)} %param.10, f32[]{:T(128)S(6)} %sub.33, f32[128]{0:T(128)S(1)} %get-tuple-element.26, f32[128]{0:T(128)S(1)} %pmax.7, f32[128]{0:T(128)S(1)} %get-tuple-element.27), kind=kLoop, calls=%fused_computation.23 | loop fusion | flops 895 | bytes 3084 | tf_op jit(solution)/shard_map/reduce_sum | solution.py:46
  57.7 0.1 dynamic-slice_negate_fusion
  57.7 1.2 multiply_convert_fusion
  58.9 0.1 collective-permute-start
  59.0 8.6 %collective-permute-done = bf16[32,8192]{1,0:T(8,128)(2,1)S(1)} collective-permute-done((bf16[32,8192]{1,0:T(8,128)(2,1)S(1)}, bf16[32,8192]{1,0:T(8,128)(2,1)S(1)}, u32[]{:S(2)}, u32[]{:S(2)}) %collective-permute-start) | collective-permute-done | bytes 524320 | tf_op jit(solution)/shard_map/ppermute | solution.py:17
  67.6 0.0 collective-permute-start.1
  67.6 0.0 all-gather.3.cloned.1.call-update
  67.6 8.6 %collective-permute-done.1 = bf16[32,8192]{1,0:T(8,128)(2,1)S(1)} collective-permute-done((bf16[32,8192]{1,0:T(8,128)(2,1)S(1)}, bf16[32,8192]{1,0:T(8,128)(2,1)S(1)}, u32[]{:S(2)}, u32[]{:S(2)}) %collective-permute-start.1) | collective-permute-done | bytes 524320 | tf_op jit(solution)/shard_map/ppermute | solution.py:17
  76.2 0.0 collective-permute-start.2
  76.2 8.6 %collective-permute-done.2 = bf16[32,8192]{1,0:T(8,128)(2,1)S(1)} collective-permute-done((bf16[32,8192]{1,0:T(8,128)(2,1)S(1)}, bf16[32,8192]{1,0:T(8,128)(2,1)S(1)}, u32[]{:S(2)}, u32[]{:S(2)}) %collective-permute-start.2) | collective-permute-done | bytes 524320 | tf_op jit(solution)/shard_map/ppermute | solution.py:17
  84.9 0.0 copy-done
  85.0 0.2 constant_dynamic-update-slice_fusion.4
  85.2 0.2 constant_dynamic-update-slice_fusion
  85.4 0.2 constant_dynamic-slice_fusion
  85.6 2.5 %copy.27 = bf16[128,8192]{0,1:T(8,128)(2,1)} copy(bf16[128,8192]{1,0:T(8,128)(2,1)S(1)} %constant_dynamic-slice_fusion) | data formatting | bytes 4194304 | tf_op jit(solution)/shard_map/jit(_roll_dynamic)/dynamic_slice | solution.py:21
  88.0 4.4 %all-to-all-start = ((bf16[128,8,1024]{0,2,1:T(8,128)(2,1)}), bf16[128,8,1024]{0,2,1:T(8,128)(2,1)}, u32[]{:S(2)}, u32[]{:S(2)}) async-start(bf16[128,8,1024]{0,2,1:T(8,128)(2,1)} %bitcast.19), calls=%async_computation | async-start | bytes 4194304 | tf_op jit(solution)/shard_map/all_to_all | solution.py:57
  93.0 67.1 %psum.39 = f32[]{:T(128)} all-reduce(f32[]{:T(128)S(6)} %neg.7), channel_id=1, replica_groups=mesh['dp'=8,'mp'=4] {'dp'}, use_global_device_ids=true, to_apply=%region_10.11 | all-reduce | flops 1 | bytes 8 | tf_op jit(solution)/shard_map/psum | solution.py:46
  160.2 30.5 %all-to-all-done = bf16[128,8,1024]{0,2,1:T(8,128)(2,1)} async-done(((bf16[128,8,1024]{0,2,1:T(8,128)(2,1)}), bf16[128,8,1024]{0,2,1:T(8,128)(2,1)}, u32[]{:S(2)}, u32[]{:S(2)}) %all-to-all-start) | async-done | bytes 2097184 | tf_op jit(solution)/shard_map/all_to_all | solution.py:57
  190.7 3.9 %copy.28 = bf16[8,128,1024]{2,1,0:T(8,128)(2,1)} copy(bf16[8,128,1024]{1,2,0:T(8,128)(2,1)} %bitcast.6) | data formatting | bytes 4194304 | tf_op jit(solution)/shard_map/all_to_all | solution.py:57
  194.6 0.0 all-gather.5.cloned.1.call-done
  194.7 3.2 %fusion = bf16[512,1024]{0,1:T(8,128)(2,1)S(1)} fusion(bf16[1024,1024]{1,0:T(8,128)(2,1)} %bitcast.20, bf16[1024,512]{1,0:T(8,128)(2,1)} %all-gather.5.cloned.1.call-done), kind=kOutput, calls=%fused_computation.3 | convolution fusion | flops 1074266112 | bytes 4194304 | tf_op jit(solution)/shard_map/dot_general | solution.py:58
  197.9 1.3 copy.29
  199.2 26.4 %all-gather.3.cloned.1.call-done = bf16[512,8192]{1,0:T(8,128)(2,1)} async-done(((bf16[512,1024]{1,0:T(8,128)(2,1)}), bf16[512,8192]{1,0:T(8,128)(2,1)}) %all-gather.3.cloned.1.call-update) | async-done | bytes 8388624 | tf_op jit(solution)/shard_map/all_gather | solution.py:53
  225.6 7.0 %convolution_convert_fusion.1 = bf16[128,512]{1,0:T(8,128)(2,1)} fusion(bf16[128,8192]{1,0:T(8,128)(2,1)S(1)} %constant_dynamic-slice_fusion, bf16[512,8192]{1,0:T(8,128)(2,1)} %all-gather.3.cloned.1.call-done), kind=kOutput, calls=%fused_computation.4 | convolution fusion | flops 1073807360 | bytes 10616832 | tf_op jit(solution)/shard_map/dot_general | solution.py:51
  (10 shorter events, 0.2 us)
Async XLA Ops:
  7.2 77.8 %copy-start = (bf16[32,8192]{1,0:T(8,128)(2,1)S(1)}, bf16[32,8192]{1,0:T(8,128)(2,1)}, u32[]{:S(2)}) copy-start(bf16[32,8192]{1,0:T(8,128)(2,1)} %param.13) | copy-start | bytes 1572868
  7.2 187.5 %all-gather.5.cloned.1.call-start = ((), (), s32[]{:S(2)}) async-start(), calls=%async_computation.2 | async-start | bytes 1179648 | tf_op jit(solution)/shard_map/all_gather | solution.py:59
  7.9 217.7 %all-gather.3.cloned.1.call-start = ((), (), s32[]{:S(2)}) async-start(), calls=%async_computation.1 | async-start | bytes 9437184 | tf_op jit(solution)/shard_map/all_gather | solution.py:53
  58.9 8.7 %collective-permute-start = (bf16[32,8192]{1,0:T(8,128)(2,1)S(1)}, bf16[32,8192]{1,0:T(8,128)(2,1)S(1)}, u32[]{:S(2)}, u32[]{:S(2)}) collective-permute-start(bf16[32,8192]{1,0:T(8,128)(2,1)S(1)} %multiply_convert_fusion), channel_id=1, source_target_pairs={{0,1},{1,2},{2,3},{3,0},{4,5},{5,6},{6,7},{7,4},{8,9},{9,10},{10,1... | collective-permute-start | bytes 1572872 | tf_op jit(solution)/shard_map/ppermute | solution.py:17
  67.6 8.6 %collective-permute-start.1 = (bf16[32,8192]{1,0:T(8,128)(2,1)S(1)}, bf16[32,8192]{1,0:T(8,128)(2,1)S(1)}, u32[]{:S(2)}, u32[]{:S(2)}) collective-permute-start(bf16[32,8192]{1,0:T(8,128)(2,1)S(1)} %collective-permute-done), channel_id=1, source_target_pairs={{0,1},{1,2},{2,3},{3,0},{4,5},{5,6},{6,7},{7,4},{8,9},{9,10},{10,1... | collective-permute-start | bytes 1572872 | tf_op jit(solution)/shard_map/ppermute | solution.py:17
  76.2 8.6 %collective-permute-start.2 = (bf16[32,8192]{1,0:T(8,128)(2,1)S(1)}, bf16[32,8192]{1,0:T(8,128)(2,1)S(1)}, u32[]{:S(2)}, u32[]{:S(2)}) collective-permute-start(bf16[32,8192]{1,0:T(8,128)(2,1)S(1)} %collective-permute-done.1), channel_id=1, source_target_pairs={{0,1},{1,2},{2,3},{3,0},{4,5},{5,6},{6,7},{7,4},{8,9},{9,10},{10,1... | collective-permute-start | bytes 1572872 | tf_op jit(solution)/shard_map/ppermute | solution.py:17
  88.0 102.7 %all-to-all-start = ((bf16[128,8,1024]{0,2,1:T(8,128)(2,1)}), bf16[128,8,1024]{0,2,1:T(8,128)(2,1)}, u32[]{:S(2)}, u32[]{:S(2)}) async-start(bf16[128,8,1024]{0,2,1:T(8,128)(2,1)} %bitcast.19), calls=%async_computation | async-start | bytes 4194304 | tf_op jit(solution)/shard_map/all_to_all | solution.py:57
Sparse Core Ops, SparseCore 0:
  10.1 43.0 all-gather.4
  67.7 157.7 all-gather.2
